TPU v7x, 32 devices: a whole 2x2x4 slice. The times are simulated.
32 devices in a mesh: inst: 4 (over x, core), dp: 4 (over z), tp: 2 (over y).
Axes of the slice: x: 2, y: 2, z: 4, core: 2. Of those that a mesh axis runs over, the one named last changes fastest.
Arguments:
- kernel_grads: bfloat16 [16, 2, 128, 4608], P(('inst', 'dp'), 'tp'), may hold values from -0.75 to 0.75
- kernel_master: float32 [2, 128, 4608], P('tp', 'dp'), may hold values from -6 to 6
- kernel_first: float32 [2, 128, 4608], P('tp', 'dp'), may hold values from -3 to 3
- kernel_second: float32 [2, 128, 4608], P('tp', 'dp'), may hold values from 0.05 to 4
- gain_grads: bfloat16 [32, 4, 4608], P(('inst', 'dp', 'tp')), may hold values from -0.29882812 to 0.29882812
- gain_master: float32 [4, 4608], replicated, may hold values from -6 to 6
- gain_first: float32 [4, 4608], replicated, may hold values from -3 to 3
- gain_second: float32 [4, 4608], replicated, may hold values from 0.05 to 4
Outputs:
- kernel_params: bfloat16 [2, 128, 4608], P('tp')
- kernel_master_new: float32 [2, 128, 4608], P('tp', 'dp')
- kernel_first_new: float32 [2, 128, 4608], P('tp', 'dp')
- kernel_second_new: float32 [2, 128, 4608], P('tp', 'dp')
- gain_params: bfloat16 [4, 4608], replicated
- gain_master_new: float32 [4, 4608], replicated
- gain_first_new: float32 [4, 4608], replicated
- gain_second_new: float32 [4, 4608], replicated
All inputs are finite; a program needn't handle non-finite values.
Results may differ from a plain program's by a relative error of at most 0.004.
Values may be sent and summed in bfloat16 or wider, within the bound.
A program may use at most 64 MiB of HBM per device.

v0:
```python
import jax
import jax.numpy as jnp
from jax import lax
from jax.sharding import PartitionSpec as P

beta_one = 0.9
beta_two = 0.95
learn_rate = 0.01
decay_rate = 0.1
epsilon = 1e-08
step_count = 100.0


def adam_update(gradient, master, first_moment, second_moment):
    first_next = beta_one * first_moment + (1.0 - beta_one) * gradient
    second_next = beta_two * second_moment + (1.0 - beta_two) * gradient * gradient
    first_hat = first_next / (1.0 - beta_one**step_count)
    second_hat = second_next / (1.0 - beta_two**step_count)
    master_next = master - learn_rate * (
        first_hat / (jnp.sqrt(second_hat) + epsilon) + decay_rate * master
    )
    return (master_next, first_next, second_next)


def local(
    kernel_grads,
    kernel_master,
    kernel_first,
    kernel_second,
    gain_grads,
    gain_master,
    gain_first,
    gain_second,
):
    local_grads = kernel_grads[0].astype(jnp.float32)
    gain_local = gain_grads[0].astype(jnp.float32)
    flat_grads = gain_local.reshape(-1)
    gain_whole = None
    partial_rows, gain_piece = (
        lax.psum_scatter(
            local_grads.astype(jnp.bfloat16), "dp", scatter_dimension=1, tiled=True
        ).astype(jnp.float32),
        lax.psum_scatter(
            flat_grads.astype(jnp.bfloat16), "dp", scatter_dimension=0, tiled=True
        ).astype(jnp.float32),
    )
    gradient, gain_piece = (
        lax.psum(partial_rows.astype(jnp.bfloat16), "inst").astype(jnp.float32),
        lax.psum(gain_piece.astype(jnp.bfloat16), "inst").astype(jnp.float32),
    )
    kernel_master_new, kernel_first_new, kernel_second_new = adam_update(
        gradient, kernel_master, kernel_first, kernel_second
    )
    kernel_params = lax.all_gather(kernel_master_new.astype(jnp.bfloat16), "dp", axis=1, tiled=True)
    gain_piece = lax.psum(gain_piece, "tp")
    gain_whole = lax.all_gather(gain_piece, "dp", axis=0, tiled=True).reshape(gain_master.shape)
    gain_master_new, gain_first_new, gain_second_new = adam_update(
        gain_whole, gain_master, gain_first, gain_second
    )
    gain_params = gain_master_new.astype(jnp.bfloat16)
    return (
        kernel_params,
        kernel_master_new,
        kernel_first_new,
        kernel_second_new,
        gain_params,
        gain_master_new,
        gain_first_new,
        gain_second_new,
    )


def solution(mesh):
    return jax.shard_map(
        local,
        mesh=mesh,
        in_specs=(
            P(("inst", "dp"), "tp", None, None),
            P("tp", "dp", None),
            P("tp", "dp", None),
            P("tp", "dp", None),
            P(("inst", "dp", "tp"), None, None),
            P(),
            P(),
            P(),
        ),
        out_specs=(
            P("tp", None, None),
            P("tp", "dp", None),
            P("tp", "dp", None),
            P("tp", "dp", None),
            P(),
            P(),
            P(),
            P(),
        ),
        check_vma=False,
    )
```

profile of v0, /device:TPU:0, one launch (start us, length us, event | category | flops | bytes accessed | tf_op | source)
XLA Modules:
  0.0 142.5 jit_solution(16182226304347898728)
XLA Ops:
  7.2 0.0 copy-start.1
  7.2 0.0 copy-start
  7.2 0.0 reduce-scatter.2.cloned.1.call-start
  7.2 0.7 reduce-scatter.2.cloned.1.call-update
  7.9 0.0 all-reduce.3.cloned.1.call-start
  8.0 34.4 %reduce-scatter.2.cloned.1.call-done = bf16[1,32,4608]{2,1,0:T(8,128)(2,1)} async-done(((bf16[1,128,4608]{2,1,0:T(8,128)(2,1)}), bf16[1,32,4608]{2,1,0:T(8,128)(2,1)}) %reduce-scatter.2.cloned.1.call-update) | async-done | bytes 294928 | tf_op jit(solution)/shard_map/reduce_scatter | solution.py:40
  42.4 0.0 all-reduce.3.cloned.1.call-update
  42.4 0.0 copy-start.5
  42.4 0.0 copy-start.6
  42.4 0.0 copy-start.2
  42.4 0.0 copy-start.3
  42.5 0.0 copy-start.4
  42.5 0.0 all-gather.3.cloned.1.call-start
  42.5 33.3 %all-reduce.3.cloned.1.call-done = bf16[1,32,4608]{2,1,0:T(8,128)(2,1)} async-done(((bf16[1,32,4608]{2,1,0:T(8,128)(2,1)}), bf16[1,32,4608]{2,1,0:T(8,128)(2,1)}) %all-reduce.3.cloned.1.call-update) | async-done | bytes 294928 | tf_op jit(solution)/shard_map/psum | solution.py:48
  75.8 0.0 copy-done.1
  75.8 0.0 copy-done
  75.8 2.7 %fusion.7 = (bf16[1,32,4608]{2,1,0:T(8,128)(2,1)}, f32[1,32,4608]{2,1,0:T(8,128)}, f32[1,32,4608]{2,1,0:T(8,128)}, f32[1,32,4608]{2,1,0:T(8,128)}) fusion(f32[1,32,4608]{2,1,0:T(8,128)S(1)} %copy-done, bf16[1,32,4608]{2,1,0:T(8,128)(2,1)} %all-reduce.3.cloned.1.call-done, f32[1,32,4608]{2,1,0:T(8,128)S(1)} %copy-done.1, f32[1,32,4608]{2,1,0:T(8,128)} %param.11), kind=kLoop, calls=%fused_computation.11 | loop fusion | flops 2506752 | bytes 4128768 | tf_op jit(solution)/shard_map/convert_element_type | solution.py:54
  78.5 0.0 all-gather.3.cloned.1.call-update
  78.6 0.0 copy-done.5
  78.6 0.0 copy-done.6
  78.6 0.6 dynamic-slice
  79.9 20.5 %all-reduce = bf16[18432]{0:T(1024)(128)(2,1)S(1)} all-reduce(bf16[18432]{0:T(1024)(128)(2,1)S(1)} %squeeze.7), channel_id=3, replica_groups=mesh['inst'=4,'dp'=4,'tp'=2] {'dp'}, use_global_device_ids=true, to_apply=%region_2.0.clone | all-reduce | flops 18432 | bytes 73728
  100.4 0.1 dynamic-slice.1
  100.5 10.9 %psum.22 = bf16[4608]{0:T(1024)(128)(2,1)S(1)} all-reduce(bf16[4608]{0:T(1024)(128)(2,1)S(1)} %dynamic-slice.1), channel_id=1, replica_groups=mesh['inst'=4,'dp'=4,'tp'=2] {'inst'}, use_global_device_ids=true, to_apply=%region_3.0 | all-reduce | flops 4608 | bytes 18432 | tf_op jit(solution)/shard_map/psum | solution.py:49
  111.4 8.2 %psum.23 = f32[4608]{0:T(1024)S(1)} all-reduce(bf16[4608]{0:T(1024)(128)(2,1)S(1)} %psum.22), channel_id=1, replica_groups=mesh['inst'=4,'dp'=4,'tp'=2] {'tp'}, use_global_device_ids=true, to_apply=%region_4.0 | all-reduce | flops 4608 | bytes 27648 | tf_op jit(solution)/shard_map/psum | solution.py:55
  119.6 13.2 %all-gather = f32[4,1,4608]{2,1,0:T(1,128)S(1)} all-gather(f32[1,1,4608]{2,1,0:T(1,128)S(1)} %reshape.22), channel_id=1, replica_groups=mesh['inst'=4,'dp'=4,'tp'=2] {'dp'}, dimensions={0}, use_global_device_ids=true | all-gather | bytes 92160 | tf_op jit(solution)/shard_map/all_gather | solution.py:56
  132.8 0.0 copy-done.2
  132.8 0.0 copy-done.3
  132.8 0.0 copy-done.4
  132.8 0.8 fusion.4
  133.6 0.0 all-gather.3.cloned.1.call-done
  133.6 2.4 %copy.23 = bf16[1,128,4608]{2,1,0:T(8,128)(2,1)} copy(bf16[1,128,4608]{2,1,0:T(8,128)(2,1)} %all-gather.3.cloned.1.call-done) | data formatting | bytes 2359296
  (2 shorter events, 0.0 us)
Async XLA Ops:
  7.2 68.6 %copy-start.1 = (f32[1,32,4608]{2,1,0:T(8,128)S(1)}, f32[1,32,4608]{2,1,0:T(8,128)}, u32[]{:S(2)}) copy-start(f32[1,32,4608]{2,1,0:T(8,128)} %param.10) | copy-start | bytes 1769476
  7.2 68.6 %copy-start = (f32[1,32,4608]{2,1,0:T(8,128)S(1)}, f32[1,32,4608]{2,1,0:T(8,128)}, u32[]{:S(2)}) copy-start(f32[1,32,4608]{2,1,0:T(8,128)} %param.9) | copy-start | bytes 1769476
  7.2 35.2 %reduce-scatter.2.cloned.1.call-start = ((), (), s32[]{:S(2)}) async-start(), calls=%async_computation.1 | async-start | bytes 1474560 | tf_op jit(solution)/shard_map/reduce_scatter | solution.py:40
  7.9 67.9 %all-reduce.3.cloned.1.call-start = ((), (), s32[]{:S(2)}) async-start(), calls=%async_computation.2 | async-start | bytes 589824 | tf_op jit(solution)/shard_map/psum | solution.py:48
  42.4 36.2 %copy-start.5 = (bf16[1,4,4608]{2,1,0:T(4,128)(2,1)S(1)}, bf16[1,4,4608]{2,1,0:T(4,128)(2,1)}, u32[]{:S(2)}) copy-start(bf16[1,4,4608]{2,1,0:T(4,128)(2,1)} %param.12) | copy-start | bytes 110596
  42.4 36.2 %copy-start.6 = (u32[32]{0:T(128)S(1)}, u32[32]{0:T(128)}, u32[]{:S(2)}) copy-start(u32[32]{0:T(128)} %constant.35) | copy-start | bytes 388
  42.4 90.3 %copy-start.2 = (f32[4,4608]{1,0:T(4,128)S(1)}, f32[4,4608]{1,0:T(4,128)}, u32[]{:S(2)}) copy-start(f32[4,4608]{1,0:T(4,128)} %param.13) | copy-start | bytes 221188
  42.4 90.3 %copy-start.3 = (f32[4,4608]{1,0:T(4,128)S(1)}, f32[4,4608]{1,0:T(4,128)}, u32[]{:S(2)}) copy-start(f32[4,4608]{1,0:T(4,128)} %param.14) | copy-start | bytes 221188
  42.5 90.3 %copy-start.4 = (f32[4,4608]{1,0:T(4,128)S(1)}, f32[4,4608]{1,0:T(4,128)}, u32[]{:S(2)}) copy-start(f32[4,4608]{1,0:T(4,128)} %param.15) | copy-start | bytes 221188
  42.5 91.1 %all-gather.3.cloned.1.call-start = ((), (), s32[]{:S(2)}) async-start(), calls=%async_computation.3 | async-start | bytes 1474560 | tf_op jit(solution)/shard_map/all_gather | solution.py:54
Sparse Core Ops, SparseCore 0:
  10.3 32.0 reduce-scatter.1
  44.7 31.0 all-reduce.2
  78.7 30.9 all-gather.2
where the time goes:
time: 143 us; the launch traced here: 142 us
  waiting for transfers between devices  68.4 us (48%)
  blocking collectives  52.8 us (37%)
  between operations  14.5 us (10%)
  other arithmetic  3.55 us (2%)
  local copies, waits for them, and re-layouts  3.1 us (2%)
    reduce_scatter x1, waiting for transfers between devices, local(): lax.psum_scatter(local_grads.astype(jnp.bfloat16), 'dp', scatter_dimensio...  34.4 us
    psum x1, waiting for transfers between devices, local(): lax.psum(partial_rows.astype(jnp.bfloat16), 'inst').astype(jnp.float32)  33.3 us
    unnamed x1, blocking collectives  20.5 us
    all_gather x1, blocking collectives, local(): lax.all_gather(gain_piece, 'dp', axis=0, tiled=True)  13.2 us
    psum x1, blocking collectives, local(): lax.psum(gain_piece.astype(jnp.bfloat16), 'inst').astype(jnp.float32)  10.9 us
    psum x1, blocking collectives, local(): gain_piece = lax.psum(gain_piece, 'tp')  8.21 us
    unnamed x18, local copies, waits for them, and re-layouts  3.08 us
  transfers between devices with their start and end apart: 3, of which 2 were waited for; matrix products, arithmetic and copies ran while one was open for 1% of the time, Pallas kernels for 0%

commit v1 on v0

--- a/solution.py
+++ b/solution.py
@@ -52,7 +52,8 @@
         gradient, kernel_master, kernel_first, kernel_second
     )
     kernel_params = lax.all_gather(kernel_master_new.astype(jnp.bfloat16), "dp", axis=1, tiled=True)
-    gain_piece = lax.psum(gain_piece, "tp")
+    terms = lax.all_gather(gain_piece, "tp")
+    gain_piece = jnp.sum(terms, axis=0)
     gain_whole = lax.all_gather(gain_piece, "dp", axis=0, tiled=True).reshape(gain_master.shape)
     gain_master_new, gain_first_new, gain_second_new = adam_update(
         gain_whole, gain_master, gain_first, gain_second

time: 143 us -> 119 us (0.83)
  waiting for transfers between devices: 68.4 us -> 51 us
  blocking collectives: 52.8 us -> 46.2 us
    psum x1, waiting for transfers between devices: 33.3 us -> 4.08 us  [local(): lax.psum(partial_rows.astype(jnp.bfloat16), 'inst').astype(jnp.float32)]
    all_gather x1, waiting for transfers between devices: 0.01 us -> 11.8 us  [local(): lax.all_gather(kernel_master_new.astype(jnp.bfloat16), 'dp', axis=1, tile...]
    psum x1 -> x0, blocking collectives: 8.21 us -> none  [local(): gain_piece = lax.psum(gain_piece, 'tp')]
    all_gather x0 -> x1, blocking collectives: none -> 4.43 us  [local(): terms = lax.all_gather(gain_piece, 'tp')]
    unnamed x1, blocking collectives: 20.5 us -> 17 us
  transfers between devices with their start and end apart: 3 -> 3, of which waited for: 2 -> 3; matrix products, arithmetic and copies ran while one was open for 1% -> 1% of each run, Pallas kernels for 0% -> 0%
where the time goes in v1:
time: 119 us
  waiting for transfers between devices  51 us (43%)
  blocking collectives  46.2 us (39%)
  between operations  14.5 us (12%)
  other arithmetic  3.62 us (3%)
  local copies, waits for them, and re-layouts  3.11 us (3%)
    reduce_scatter x1, waiting for transfers between devices, local(): lax.psum_scatter(local_grads.astype(jnp.bfloat16), 'dp', scatter_dimensio...  34.4 us
    unnamed x1, blocking collectives  17 us
    all_gather x1, blocking collectives, local(): lax.all_gather(gain_piece, 'dp', axis=0, tiled=True)  13.9 us
    all_gather x1, waiting for transfers between devices, local(): lax.all_gather(kernel_master_new.astype(jnp.bfloat16), 'dp', axis=1, tile...  11.8 us
    psum x1, blocking collectives, local(): lax.psum(gain_piece.astype(jnp.bfloat16), 'inst').astype(jnp.float32)  10.8 us
    all_gather x1, blocking collectives, local(): terms = lax.all_gather(gain_piece, 'tp')  4.43 us
    psum x1, waiting for transfers between devices, local(): lax.psum(partial_rows.astype(jnp.bfloat16), 'inst').astype(jnp.float32)  4.08 us
    unnamed x18, local copies, waits for them, and re-layouts  3.08 us
  transfers between devices with their start and end apart: 3, of which 3 were waited for; matrix products, arithmetic and copies ran while one was open for 1% of the time, Pallas kernels for 0%

profile of v1, /device:TPU:0, one launch (start us, length us, event | category | flops | bytes accessed | tf_op | source)
XLA Modules:
  0.0 118.5 jit_solution(13353519362853990028)
XLA Ops:
  7.2 0.0 copy-start.6
  7.2 0.0 copy-start.5
  7.2 0.0 copy-start.1
  7.2 0.0 copy-start
  7.2 0.0 reduce-scatter.2.cloned.1.call-start
  7.3 0.7 reduce-scatter.2.cloned.1.call-update
  7.9 0.0 all-reduce.3.cloned.1.call-start
  8.0 34.4 %reduce-scatter.2.cloned.1.call-done = bf16[1,32,4608]{2,1,0:T(8,128)(2,1)} async-done(((bf16[1,128,4608]{2,1,0:T(8,128)(2,1)}), bf16[1,32,4608]{2,1,0:T(8,128)(2,1)}) %reduce-scatter.2.cloned.1.call-update) | async-done | bytes 294928 | tf_op jit(solution)/shard_map/reduce_scatter | solution.py:40
  42.4 0.0 all-reduce.3.cloned.1.call-update
  42.4 0.0 all-gather.4.cloned.1.call-start
  42.5 0.0 copy-done.5
  42.5 0.0 copy-done.6
  42.5 0.6 dynamic-slice
  43.8 17.0 %all-reduce = bf16[18432]{0:T(1024)(128)(2,1)S(1)} all-reduce(bf16[18432]{0:T(1024)(128)(2,1)S(1)} %squeeze.7), channel_id=3, replica_groups=mesh['inst'=4,'dp'=4,'tp'=2] {'dp'}, use_global_device_ids=true, to_apply=%region_2.0.clone | all-reduce | flops 18432 | bytes 73728
  60.8 0.1 dynamic-slice.1
  60.9 10.8 %psum.15 = bf16[1,4608]{1,0:T(2,128)(2,1)S(1)} all-reduce(bf16[1,4608]{1,0:T(2,128)(2,1)S(1)} %all_gather.16), channel_id=1, replica_groups=mesh['inst'=4,'dp'=4,'tp'=2] {'inst'}, use_global_device_ids=true, to_apply=%region_3.0 | all-reduce | flops 4608 | bytes 18432 | tf_op jit(solution)/shard_map/psum | solution.py:49
  71.7 0.0 copy-start.2
  71.7 0.0 copy-start.4
  71.7 4.1 %all-reduce.3.cloned.1.call-done = bf16[1,32,4608]{2,1,0:T(8,128)(2,1)} async-done(((bf16[1,32,4608]{2,1,0:T(8,128)(2,1)}), bf16[1,32,4608]{2,1,0:T(8,128)(2,1)}) %all-reduce.3.cloned.1.call-update) | async-done | bytes 294928 | tf_op jit(solution)/shard_map/psum | solution.py:48
  75.8 0.0 copy-done.1
  75.8 0.0 copy-done
  75.8 2.7 %fusion.7 = (bf16[1,32,4608]{2,1,0:T(8,128)(2,1)}, f32[1,32,4608]{2,1,0:T(8,128)}, f32[1,32,4608]{2,1,0:T(8,128)}, f32[1,32,4608]{2,1,0:T(8,128)}) fusion(f32[1,32,4608]{2,1,0:T(8,128)S(1)} %copy-done, bf16[1,32,4608]{2,1,0:T(8,128)(2,1)} %all-reduce.3.cloned.1.call-done, f32[1,32,4608]{2,1,0:T(8,128)S(1)} %copy-done.1, f32[1,32,4608]{2,1,0:T(8,128)} %param.11), kind=kLoop, calls=%fused_computation.12 | loop fusion | flops 2506752 | bytes 4128768 | tf_op jit(solution)/shard_map/convert_element_type | solution.py:54
  78.6 0.0 all-gather.4.cloned.1.call-update
  78.6 4.4 %all-gather = f32[2,1,4608]{2,1,0:T(1,128)S(1)} all-gather(f32[1,1,4608]{2,1,0:T(1,128)S(1)} %bitcast_convert_fusion), channel_id=1, replica_groups=mesh['inst'=4,'dp'=4,'tp'=2] {'tp'}, dimensions={0}, use_global_device_ids=true | all-gather | bytes 55296 | tf_op jit(solution)/shard_map/all_gather | solution.py:55
  83.0 0.1 reduce_sum.9
  83.1 13.9 %all-gather.1 = f32[4,1,4608]{2,1,0:T(1,128)S(1)} all-gather(f32[1,1,4608]{2,1,0:T(1,128)S(1)} %reshape.24), channel_id=1, replica_groups=mesh['inst'=4,'dp'=4,'tp'=2] {'dp'}, dimensions={0}, use_global_device_ids=true | all-gather | bytes 92160 | tf_op jit(solution)/shard_map/all_gather | solution.py:57
  97.0 0.0 copy-done.2
  97.0 0.0 copy-done.3
  97.0 0.0 copy-done.4
  97.1 0.8 fusion.4
  97.9 11.8 %all-gather.4.cloned.1.call-done = bf16[1,128,4608]{2,1,0:T(8,128)(2,1)} async-done(((bf16[1,32,4608]{2,1,0:T(8,128)(2,1)}), bf16[1,128,4608]{2,1,0:T(8,128)(2,1)}) %all-gather.4.cloned.1.call-update) | async-done | bytes 1179664 | tf_op jit(solution)/shard_map/all_gather | solution.py:54
  109.6 2.4 %copy.23 = bf16[1,128,4608]{2,1,0:T(8,128)(2,1)} copy(bf16[1,128,4608]{2,1,0:T(8,128)(2,1)} %all-gather.4.cloned.1.call-done) | data formatting | bytes 2359296
  (5 shorter events, 0.1 us)
Async XLA Ops:
  7.2 35.4 %copy-start.6 = (u32[32]{0:T(128)S(1)}, u32[32]{0:T(128)}, u32[]{:S(2)}) copy-start(u32[32]{0:T(128)} %constant.37) | copy-start | bytes 388
  7.2 35.3 %copy-start.5 = (bf16[1,4,4608]{2,1,0:T(4,128)(2,1)S(1)}, bf16[1,4,4608]{2,1,0:T(4,128)(2,1)}, u32[]{:S(2)}) copy-start(bf16[1,4,4608]{2,1,0:T(4,128)(2,1)} %param.12) | copy-start | bytes 110596
  7.2 68.6 %copy-start.1 = (f32[1,32,4608]{2,1,0:T(8,128)S(1)}, f32[1,32,4608]{2,1,0:T(8,128)}, u32[]{:S(2)}) copy-start(f32[1,32,4608]{2,1,0:T(8,128)} %param.10) | copy-start | bytes 1769476
  7.2 68.6 %copy-start = (f32[1,32,4608]{2,1,0:T(8,128)S(1)}, f32[1,32,4608]{2,1,0:T(8,128)}, u32[]{:S(2)}) copy-start(f32[1,32,4608]{2,1,0:T(8,128)} %param.9) | copy-start | bytes 1769476
  7.2 35.2 %reduce-scatter.2.cloned.1.call-start = ((), (), s32[]{:S(2)}) async-start(), calls=%async_computation.1 | async-start | bytes 1474560 | tf_op jit(solution)/shard_map/reduce_scatter | solution.py:40
  7.9 67.9 %all-reduce.3.cloned.1.call-start = ((), (), s32[]{:S(2)}) async-start(), calls=%async_computation.2 | async-start | bytes 589824 | tf_op jit(solution)/shard_map/psum | solution.py:48
  42.4 67.2 %all-gather.4.cloned.1.call-start = ((), (), s32[]{:S(2)}) async-start(), calls=%async_computation.3 | async-start | bytes 1474560 | tf_op jit(solution)/shard_map/all_gather | solution.py:54
  71.7 25.3 %copy-start.2 = (f32[4,4608]{1,0:T(4,128)S(1)}, f32[4,4608]{1,0:T(4,128)}, u32[]{:S(2)}) copy-start(f32[4,4608]{1,0:T(4,128)} %param.13) | copy-start | bytes 221188
  71.7 25.3 %copy-start.3 = (f32[4,4608]{1,0:T(4,128)S(1)}, f32[4,4608]{1,0:T(4,128)}, u32[]{:S(2)}) copy-start(f32[4,4608]{1,0:T(4,128)} %param.14) | copy-start | bytes 221188
  71.7 25.3 %copy-start.4 = (f32[4,4608]{1,0:T(4,128)S(1)}, f32[4,4608]{1,0:T(4,128)}, u32[]{:S(2)}) copy-start(f32[4,4608]{1,0:T(4,128)} %param.15) | copy-start | bytes 221188
Sparse Core Ops, SparseCore 0:
  10.3 32.0 reduce-scatter.1
  44.7 31.0 all-reduce.2
  78.7 30.9 all-gather.3
